TPU v7x, 32 devices: a whole 2x2x4 slice. The times are simulated.
32 devices in a mesh: blk: 4 (over y, x), grp: 8 (over z, core).
Axes of the slice: x: 2, y: 2, z: 4, core: 2. Of those that a mesh axis runs over, the one named last changes fastest.
Arguments:
- points: float32 [3, 4096], P(None, ('blk', 'grp')), may hold values from 0 to 1
- labels: int32 [4096], P(('blk', 'grp')), may hold values 0 or 1
- shape_scale: float32 [4096], P(('blk', 'grp')), may hold values from 0.1 to 0.4
- krylov_basis: float32 [8, 32, 4096], P(None, None, ('blk', 'grp')), may hold values from -6 to 6
- sketch: float32 [1024, 4096], P(None, ('blk', 'grp')), may hold values from -0.09375 to 0.09375
- sketched_basis: float32 [8, 32, 1024], replicated, may hold values from -0.1875 to 0.1875
Outputs:
- next_vector: float32 [32, 4096], P(None, ('blk', 'grp'))
- coefficients: float32 [8, 32], replicated
- sketch_next: float32 [32, 1024], replicated
- norms: float32 [32], replicated
All inputs are finite; a program needn't handle non-finite values. No bound on the sum of `labels` on one device may be relied on, other than what follows from the above.
Results may differ from a plain program's by a relative error of at most 0.0003.
Values sent between devices are 32-bit elements; how exact they have to be, the bound alone decides.
A program may use at most 64 MiB of HBM per device.

v0:
```python
import math
import jax
import jax.numpy as jnp
from jax import lax
from jax.sharding import PartitionSpec as P

SYSTEMS = 32
KRYLOV = 8


def kernel_terms(target_points, target_labels, source_block):
    source_points = source_block[0:3]
    scales = source_block[3]
    weights_block = source_block[4:]
    delta_x = source_points[0][:, None] - target_points[0][None, :]
    delta_y = source_points[1][:, None] - target_points[1][None, :]
    delta_z = source_points[2][:, None] - target_points[2][None, :]
    radius_sq = delta_x * delta_x + delta_y * delta_y + delta_z * delta_z
    squared_scale = (scales * scales)[:, None]
    shifted = radius_sq + squared_scale
    inverse = lax.rsqrt(shifted)
    boundary = shifted * inverse
    interior = (3.0 * squared_scale + 2.0 * radius_sq) * inverse * inverse * inverse
    kernel = jnp.where(target_labels[None, :] == 1, interior, boundary)
    return jnp.dot(
        weights_block, kernel, precision=lax.Precision.HIGHEST, preferred_element_type=jnp.float32
    )


def block_size(length, wanted):
    return wanted if length % wanted == 0 else length


def accumulate(running, target_points, target_labels, source_block):
    target_count = target_points.shape[1]
    source_count = source_block.shape[1]
    tblock = block_size(target_count, 2048)
    sblock = block_size(source_count, 2048)
    system_rows = running.shape[0]

    def over_targets(target_index, current):

        def over_sources(source_index, partial_value):
            portion = lax.dynamic_slice_in_dim(source_block, source_index * sblock, sblock, 1)
            return partial_value + kernel_terms(target_points, target_labels, portion)

        partial_value = lax.fori_loop(
            0, source_count // sblock, over_sources, jnp.zeros((system_rows, tblock), jnp.float32)
        )
        return current + partial_value

    return lax.fori_loop(0, target_count // tblock, over_targets, running)


def shards(points, labels, shape_scale, krylov_basis, sketch, sketched_basis):
    own_count = points.shape[1]
    everything = lax.axis_size("blk") * lax.axis_size("grp") * own_count
    sources = jnp.concatenate([points, shape_scale[None, :], krylov_basis[KRYLOV - 1]], axis=0)
    empty = jnp.zeros((SYSTEMS, own_count), jnp.float32)
    summed = accumulate(
        empty, points, labels, lax.all_gather(sources, ("blk", "grp"), axis=1, tiled=True)
    )
    image = summed / math.sqrt(everything)
    local_sketch = lax.dot_general(
        image,
        sketch,
        (((1,), (1,)), ((), ())),
        precision=lax.Precision.HIGHEST,
        preferred_element_type=jnp.float32,
    )
    sketched = lax.psum(local_sketch, ("blk", "grp"))
    coefficients = jnp.einsum(
        "jrk,rk->jr", sketched_basis, sketched, precision=lax.Precision.HIGHEST
    )
    remainder = sketched - jnp.einsum(
        "jr,jrk->rk", coefficients, sketched_basis, precision=lax.Precision.HIGHEST
    )
    norms = jnp.sqrt(jnp.mean(remainder * remainder, axis=1) + 1e-06)
    sketch_next = remainder / norms[:, None]
    reduced = image - jnp.einsum(
        "jr,jrn->rn", coefficients, krylov_basis, precision=lax.Precision.HIGHEST
    )
    next_vector = reduced / norms[:, None]
    return (next_vector, coefficients, sketch_next, norms)


def solution(mesh):
    placed = (
        P(None, ("blk", "grp")),
        P(("blk", "grp")),
        P(("blk", "grp")),
        P(None, None, ("blk", "grp")),
        P(None, ("blk", "grp")),
        P(),
    )
    return jax.shard_map(
        shards,
        mesh=mesh,
        in_specs=placed,
        out_specs=(P(None, ("blk", "grp")), P(), P(), P()),
        check_vma=False,
    )
```

profile of v0, /device:TPU:0, one launch (start us, length us, event | category | flops | bytes accessed | tf_op | source)
XLA Modules:
  0.0 195.9 jit_solution(17373773227067051160)
XLA Ops:
  7.2 0.0 copy-start
  7.2 0.0 all-reduce.2.cloned.1.call-start
  7.2 0.0 copy-start.4
  7.2 0.8 slice_bitcast_fusion.3
  8.0 0.0 copy-start.7
  8.1 0.0 copy-done.4
  8.1 0.7 copy-done.7
  8.7 45.9 %all_gather.3 = f32[36,4096]{1,0:T(8,128)S(1)} all-gather(f32[36,128]{1,0:T(8,128)S(1)} %pad_maximum_fusion), channel_id=1, replica_groups=mesh['blk'=4,'grp'=8] {'blk','grp'}, dimensions={1}, use_global_device_ids=true | all-gather | bytes 608256 | tf_op jit(solution)/shard_map/all_gather | solution.py:61
  54.7 0.0 copy-done.8
  54.7 4.4 %while.21 = (s32[]{:T(128)}, f32[32,128]{1,0:T(8,128)S(1)}, f32[36,4096]{1,0:T(8,128)S(1)}, s32[128]{0:T(128)S(1)}, f32[3,128]{1,0:T(4,128)S(1)}, /*index=5*/s32...) while((s32[]{:T(128)}, f32[32,128]{1,0:T(8,128)S(1)}, ...), condition=%wide.region_1.0_spmd.clone, body=%wide.region_0.1_spmd.clone.sunk | while | flops 104870024 | bytes 423813 | solution.py:47
  54.7 0.1 constant_dynamic-slice_fusion.2
  54.8 2.0 %convolution_add_fusion.2 = f32[32,128]{1,0:T(8,128)S(1)} fusion(f32[2048]{0:T(1024)S(1)} %bitcast.42, f32[128]{0:T(128)S(1)} %get-tuple-element.195, f32[2048]{0:T(1024)S(1)} %bitcast.45, f32[128]{0:T(128)S(1)} %get-tuple-element.197, f32[2048]{0:T(1024)S(1)} %bitcast.44, f32[128]{0:T(128)S(1)} %get-tuple-element.199, f32[2048]{0:T(1024)S(1)} %bitcast.43, ...), kind=kOutput, calls=%fused_computation.2.clone.1 | convolution fusion | flops 104865792 | bytes 337929 | tf_op jit(solution)/shard_map/while/body/eval_jaxpr/while/body/eval_jaxpr/dot_general | solution.py:25
  56.9 0.1 constant_dynamic-slice_fusion.2
  57.0 2.0 %convolution_add_fusion.2 = f32[32,128]{1,0:T(8,128)S(1)} fusion(f32[2048]{0:T(1024)S(1)} %bitcast.42, f32[128]{0:T(128)S(1)} %get-tuple-element.195, f32[2048]{0:T(1024)S(1)} %bitcast.45, f32[128]{0:T(128)S(1)} %get-tuple-element.197, f32[2048]{0:T(1024)S(1)} %bitcast.44, f32[128]{0:T(128)S(1)} %get-tuple-element.199, f32[2048]{0:T(1024)S(1)} %bitcast.43, ...), kind=kOutput, calls=%fused_computation.2.clone.1 | convolution fusion | flops 104865792 | bytes 337929 | tf_op jit(solution)/shard_map/while/body/eval_jaxpr/while/body/eval_jaxpr/dot_general | solution.py:25
  59.1 0.0 copy-done.2
  59.1 1.3 fusion.32
  60.3 0.0 all-reduce.2.cloned.1.call-update
  60.4 120.9 %all-reduce.2.cloned.1.call-done = f32[32,1024]{1,0:T(8,128)} async-done(((f32[32,1024]{1,0:T(8,128)}), f32[32,1024]{1,0:T(8,128)}) %all-reduce.2.cloned.1.call-update) | async-done | bytes 131088 | tf_op jit(solution)/shard_map/psum | solution.py:71
  181.2 0.0 copy-done
  181.3 3.6 %fusion.27 = f32[32,1,8]{2,1,0:T(1,128)S(1)} fusion(f32[8,32,1024]{2,1,0:T(8,128)S(1)} %copy-done, f32[32,1024,1]{1,0,2:T(8,128)} %bitcast.40), kind=kOutput, calls=%fused_computation.36 | convolution fusion | flops 3145728 | bytes 1180672 | tf_op jit(solution)/shard_map/jrk,rk->jr/dot_general | solution.py:72
  184.8 0.1 copy.12
  184.9 0.1 copy.13
  185.0 0.5 copy-done.5
  185.5 0.0 copy-done.3
  185.5 0.4 fusion.29
  185.9 0.0 copy-start.1
  185.9 1.5 fusion.25
  187.4 0.0 copy-done.1
  187.4 0.1 multiply_reduce_fusion
  187.6 0.7 subtract_divide_fusion
  188.3 0.0 copy-done.6
  188.3 0.7 broadcast_divide_fusion
  (14 shorter events, 0.1 us)
Async XLA Ops:
  7.2 174.1 %copy-start = (f32[8,32,1024]{2,1,0:T(8,128)S(1)}, f32[8,32,1024]{2,1,0:T(8,128)}, u32[]{:S(2)}) copy-start(f32[8,32,1024]{2,1,0:T(8,128)} %param.13) | copy-start | bytes 3145732
  7.2 174.1 %all-reduce.2.cloned.1.call-start = ((), (), s32[]{:S(2)}) async-start(), calls=%async_computation | async-start | bytes 262144 | tf_op jit(solution)/shard_map/psum | solution.py:71
  7.2 0.8 copy-start.4
  8.0 0.7 copy-start.7
  8.7 46.0 %copy-start.8 = (s32[128]{0:T(128)S(1)}, s32[128]{0:T(128)}, u32[]{:S(2)}) copy-start(s32[128]{0:T(128)} %param.9) | copy-start | bytes 1540
  54.7 4.4 %copy-start.2 = (f32[1024,128]{1,0:T(8,128)S(1)}, f32[1024,128]{1,0:T(8,128)}, u32[]{:S(2)}) copy-start(f32[1024,128]{1,0:T(8,128)} %param.12) | copy-start | bytes 1572868
  181.2 4.3 %copy-start.3 = (f32[8,32,128]{2,1,0:T(8,128)S(1)}, f32[8,32,128]{2,1,0:T(8,128)}, u32[]{:S(2)}) copy-start(f32[8,32,128]{2,1,0:T(8,128)} %param.11) | copy-start | bytes 393220
  184.9 0.6 copy-start.5
  185.9 1.5 copy-start.1
  187.6 0.7 copy-start.6
Sparse Core Ops, SparseCore 0:
  60.5 120.7 all-reduce.1
where the time goes:
time: 196 us
  waiting for transfers between devices  121 us (62%)
  blocking collectives  45.9 us (23%)
  between operations  14.1 us (7%)
  matrix products  10.7 us (5%)
  local copies, waits for them, and re-layouts  2.17 us (1%)
    psum x1, waiting for transfers between devices, shards(): sketched = lax.psum(local_sketch, ('blk', 'grp'))  121 us
    all_gather x1, blocking collectives, shards(): lax.all_gather(sources, ('blk', 'grp'), axis=1, tiled=True)  45.9 us
    dot_general x2, matrix products, kernel_terms(): jnp.dot(weights_block, kernel, precision=lax.Precision.HIGHEST, preferred...  4 us
  transfers between devices with their start and end apart: 1, of which 1 were waited for; matrix products, arithmetic and copies ran while one was open for 0% of the time, Pallas kernels for 0%

commit v1 on v0

--- a/solution.py
+++ b/solution.py
@@ -68,7 +68,7 @@
         precision=lax.Precision.HIGHEST,
         preferred_element_type=jnp.float32,
     )
-    sketched = lax.psum(local_sketch, ("blk", "grp"))
+    sketched = lax.psum(lax.psum(local_sketch, "grp"), "blk")
     coefficients = jnp.einsum(
         "jrk,rk->jr", sketched_basis, sketched, precision=lax.Precision.HIGHEST
     )

time: 196 us -> 171 us (0.87)
  waiting for transfers between devices: 121 us -> 95.5 us
    psum x1 -> x2, waiting for transfers between devices: 121 us -> 95.5 us  [shards(): sketched = lax.psum(lax.psum(local_sketch, 'grp'), 'blk')]
  transfers between devices with their start and end apart: 1 -> 2, of which waited for: 1 -> 2; matrix products, arithmetic and copies ran while one was open for 0% -> 0% of each run, Pallas kernels for 0% -> 0%
where the time goes in v1:
time: 171 us
  waiting for transfers between devices  95.5 us (56%)
  blocking collectives  45.9 us (27%)
  between operations  14.1 us (8%)
  matrix products  10.7 us (6%)
  local copies, waits for them, and re-layouts  2.17 us (1%)
  other arithmetic  1.87 us (1%)
    psum x2, waiting for transfers between devices, shards(): sketched = lax.psum(lax.psum(local_sketch, 'grp'), 'blk')  95.5 us
    all_gather x1, blocking collectives, shards(): lax.all_gather(sources, ('blk', 'grp'), axis=1, tiled=True)  45.9 us
    dot_general x2, matrix products, kernel_terms(): jnp.dot(weights_block, kernel, precision=lax.Precision.HIGHEST, preferred...  4 us
    dot_general x1, matrix products, shards(): jnp.einsum('jrk,rk->jr', sketched_basis, sketched, precision=lax.Precisio...  3.57 us
  transfers between devices with their start and end apart: 2, of which 2 were waited for; matrix products, arithmetic and copies ran while one was open for 0% of the time, Pallas kernels for 0%

profile of v1, /device:TPU:0, one launch (start us, length us, event | category | flops | bytes accessed | tf_op | source)
XLA Modules:
  0.0 170.5 jit_solution(13232438662401297790)
XLA Ops:
  7.2 0.0 copy-start
  7.2 0.0 all-reduce.3.cloned.1.call-start
  7.2 0.0 copy-start.4
  7.2 0.8 slice_bitcast_fusion.3
  8.1 0.0 copy-done.4
  8.1 0.7 copy-done.7
  8.7 45.9 %all_gather.3 = f32[36,4096]{1,0:T(8,128)S(1)} all-gather(f32[36,128]{1,0:T(8,128)S(1)} %pad_maximum_fusion), channel_id=1, replica_groups=mesh['blk'=4,'grp'=8] {'blk','grp'}, dimensions={1}, use_global_device_ids=true | all-gather | bytes 608256 | tf_op jit(solution)/shard_map/all_gather | solution.py:61
  54.7 0.0 copy-done.8
  54.7 4.4 %while.21 = (s32[]{:T(128)}, f32[32,128]{1,0:T(8,128)S(1)}, f32[36,4096]{1,0:T(8,128)S(1)}, s32[128]{0:T(128)S(1)}, f32[3,128]{1,0:T(4,128)S(1)}, /*index=5*/s32...) while((s32[]{:T(128)}, f32[32,128]{1,0:T(8,128)S(1)}, ...), condition=%wide.region_1.0_spmd.clone, body=%wide.region_0.1_spmd.clone.sunk | while | flops 104870024 | bytes 423813 | solution.py:47
  54.7 0.1 constant_dynamic-slice_fusion.2
  54.8 2.0 %convolution_add_fusion.2 = f32[32,128]{1,0:T(8,128)S(1)} fusion(f32[2048]{0:T(1024)S(1)} %bitcast.42, f32[128]{0:T(128)S(1)} %get-tuple-element.195, f32[2048]{0:T(1024)S(1)} %bitcast.45, f32[128]{0:T(128)S(1)} %get-tuple-element.197, f32[2048]{0:T(1024)S(1)} %bitcast.44, f32[128]{0:T(128)S(1)} %get-tuple-element.199, f32[2048]{0:T(1024)S(1)} %bitcast.43, ...), kind=kOutput, calls=%fused_computation.2.clone.1 | convolution fusion | flops 104865792 | bytes 337929 | tf_op jit(solution)/shard_map/while/body/eval_jaxpr/while/body/eval_jaxpr/dot_general | solution.py:25
  56.9 0.1 constant_dynamic-slice_fusion.2
  57.0 2.0 %convolution_add_fusion.2 = f32[32,128]{1,0:T(8,128)S(1)} fusion(f32[2048]{0:T(1024)S(1)} %bitcast.42, f32[128]{0:T(128)S(1)} %get-tuple-element.195, f32[2048]{0:T(1024)S(1)} %bitcast.45, f32[128]{0:T(128)S(1)} %get-tuple-element.197, f32[2048]{0:T(1024)S(1)} %bitcast.44, f32[128]{0:T(128)S(1)} %get-tuple-element.199, f32[2048]{0:T(1024)S(1)} %bitcast.43, ...), kind=kOutput, calls=%fused_computation.2.clone.1 | convolution fusion | flops 104865792 | bytes 337929 | tf_op jit(solution)/shard_map/while/body/eval_jaxpr/while/body/eval_jaxpr/dot_general | solution.py:25
  59.1 0.0 copy-done.2
  59.1 1.3 fusion.32
  60.3 0.0 all-reduce.3.cloned.1.call-update
  60.4 0.0 all-reduce.5.cloned.1.call-start
  60.4 51.3 %all-reduce.3.cloned.1.call-done = f32[32,1024]{1,0:T(8,128)} async-done(((f32[32,1024]{1,0:T(8,128)}), f32[32,1024]{1,0:T(8,128)}) %all-reduce.3.cloned.1.call-update) | async-done | bytes 131088 | tf_op jit(solution)/shard_map/psum | solution.py:71
  111.7 0.0 all-reduce.5.cloned.1.call-update
  111.7 44.2 %all-reduce.5.cloned.1.call-done = f32[32,1024]{1,0:T(8,128)} async-done(((f32[32,1024]{1,0:T(8,128)}), f32[32,1024]{1,0:T(8,128)}) %all-reduce.5.cloned.1.call-update) | async-done | bytes 131088 | tf_op jit(solution)/shard_map/psum | solution.py:71
  155.9 0.0 copy-done
  155.9 3.6 %fusion.27 = f32[32,1,8]{2,1,0:T(1,128)S(1)} fusion(f32[8,32,1024]{2,1,0:T(8,128)S(1)} %copy-done, f32[32,1024,1]{1,0,2:T(8,128)} %bitcast.40), kind=kOutput, calls=%fused_computation.36 | convolution fusion | flops 3145728 | bytes 1180672 | tf_op jit(solution)/shard_map/jrk,rk->jr/dot_general | solution.py:72
  159.5 0.1 copy.12
  159.5 0.1 copy.13
  159.6 0.5 copy-done.5
  160.1 0.0 copy-done.3
  160.1 0.4 fusion.29
  160.6 1.5 fusion.25
  162.1 0.1 multiply_reduce_fusion
  162.2 0.7 subtract_divide_fusion
  162.9 0.0 copy-done.6
  162.9 0.7 broadcast_divide_fusion
  (17 shorter events, 0.1 us)
Async XLA Ops:
  7.2 148.7 %copy-start = (f32[8,32,1024]{2,1,0:T(8,128)S(1)}, f32[8,32,1024]{2,1,0:T(8,128)}, u32[]{:S(2)}) copy-start(f32[8,32,1024]{2,1,0:T(8,128)} %param.13) | copy-start | bytes 3145732
  7.2 104.5 %all-reduce.3.cloned.1.call-start = ((), (), s32[]{:S(2)}) async-start(), calls=%async_computation | async-start | bytes 262144 | tf_op jit(solution)/shard_map/psum | solution.py:71
  7.2 0.8 copy-start.4
  8.0 0.7 copy-start.7
  8.7 46.0 %copy-start.8 = (s32[128]{0:T(128)S(1)}, s32[128]{0:T(128)}, u32[]{:S(2)}) copy-start(s32[128]{0:T(128)} %param.9) | copy-start | bytes 1540
  54.7 4.4 %copy-start.2 = (f32[1024,128]{1,0:T(8,128)S(1)}, f32[1024,128]{1,0:T(8,128)}, u32[]{:S(2)}) copy-start(f32[1024,128]{1,0:T(8,128)} %param.12) | copy-start | bytes 1572868
  60.4 95.5 %all-reduce.5.cloned.1.call-start = ((), (), s32[]{:S(2)}) async-start(), calls=%async_computation.1 | async-start | bytes 262144 | tf_op jit(solution)/shard_map/psum | solution.py:71
  155.9 4.3 %copy-start.3 = (f32[8,32,128]{2,1,0:T(8,128)S(1)}, f32[8,32,128]{2,1,0:T(8,128)}, u32[]{:S(2)}) copy-start(f32[8,32,128]{2,1,0:T(8,128)} %param.11) | copy-start | bytes 393220
  159.5 0.6 copy-start.5
  160.6 1.5 copy-start.1
  162.2 0.7 copy-start.6
Sparse Core Ops, SparseCore 0:
  60.5 51.1 all-reduce.2
  114.6 41.2 all-reduce.4
